TPU v7x, 128 devices: a whole 4x4x4 slice. The times are simulated.
128 devices in a mesh: scen: 32 (over z, y_lo, x), fac: 4 (over y_hi, core).
Axes of the slice: x: 4, y: 4 (y_hi: 2, y_lo: 2; y = y_hi * 2 + y_lo), z: 4, core: 2. Of those that a mesh axis runs over, the one named last changes fastest.
Arguments:
- scenario_draws: bfloat16 [32768, 4096], P('scen'), may hold values from -6 to 6
- cholesky: bfloat16 [4096, 4096], P('scen', 'fac'), may hold values from -1.5 to 1.5, as said below
- exposures: bfloat16 [4096, 4096], P('fac'), may hold values from -0.09375 to 0.09375
- drift: float32 [4096], P('fac'), may hold values from -3 to 3
Outputs:
- covariance: float32 [4096, 4096], P('scen', 'fac')
- expected: float32 [4096], P('fac')
Inputs may be any that keep to these rules, and one draw needn't show every extreme that they name: cholesky is lower triangular (zero above the diagonal) with diagonal entries of 0.5 to 1.5.
All inputs are finite; a program needn't handle non-finite values.
Results may differ from a plain program's by a relative error of at most 0.0013.
Values may be sent and summed in bfloat16 or wider, within the bound.
No kernel may reach another device: no remote copies, remote signals or barrier semaphores. Data moves between devices by JAX's collectives and lax.ppermute only.
A program may use at most 128 MiB of HBM per device.

v0:
```python
import jax
import jax.numpy as jnp
from jax import lax
from jax.sharding import Mesh
from jax.sharding import PartitionSpec as P

SCEN = ("scen_0", "scen_1", "scen_2")


def in_order(tiles, dim):
    tiles = jnp.moveaxis(tiles, 0, dim)
    shape = tiles.shape
    return tiles.reshape(*shape[:dim], shape[dim] * shape[dim + 1], *shape[dim + 2 :])


def gather_in_order(x, axes, order):
    tiles = x
    for k in order:
        tiles = lax.all_gather(tiles, axes[k])
    done = order[::-1]
    back = [done.index(k) for k in range(len(axes))]
    tiles = tiles.transpose(*back, *range(len(axes), tiles.ndim))
    return tiles.reshape(-1, *x.shape)


def whole_of(x, axes, order, dim):
    return in_order(gather_in_order(x, axes, order), dim)


def from_everyone(x, axis):
    copies = jnp.broadcast_to(x, (lax.axis_size(axis), *x.shape))
    return lax.all_to_all(copies, axis, split_axis=0, concat_axis=0, tiled=True)


def over_copies(x, axis):
    return from_everyone(x, axis).sum(axis=0)


def on_device(scenario_draws, cholesky, exposures, drift):
    count_rows = scenario_draws.shape[0]
    own_desks = exposures.shape[0]
    mixed = jnp.dot(
        scenario_draws, whole_of(cholesky, SCEN, (1, 0, 2), 0), preferred_element_type=jnp.float32
    )
    shocks = (mixed + drift[None, :]).astype(jnp.bfloat16)
    pnl_acc = lax.dot_general(
        lax.all_gather(shocks, "fac", axis=1, tiled=True),
        exposures,
        (((1,), (1,)), ((), ())),
        preferred_element_type=jnp.float32,
    )
    pnl = pnl_acc.astype(jnp.bfloat16)
    gathered = lax.all_gather(pnl, "fac", axis=1, tiled=True)
    desk_total = gathered.shape[1]
    column_sums = over_copies(jnp.sum(gathered, axis=0, dtype=jnp.float32), SCEN)
    scenario_total = count_rows * lax.axis_size(SCEN)
    means = column_sums / scenario_total
    col_means = lax.dynamic_slice_in_dim(means, lax.axis_index("fac") * own_desks, own_desks, 0)
    owned_rows = desk_total // lax.axis_size(SCEN)
    row_start = lax.axis_index(SCEN) * owned_rows
    block = lax.psum_scatter(
        lax.dot_general(
            gathered, pnl, (((0,), (0,)), ((), ())), preferred_element_type=jnp.float32
        ),
        SCEN,
        scatter_dimension=0,
        tiled=True,
    )
    row_means = lax.dynamic_slice_in_dim(means, row_start, owned_rows, 0)
    covariance = (block - scenario_total * row_means[:, None] * col_means[None, :]) / (
        scenario_total - 1
    )
    return (covariance, col_means)


def solution(mesh):
    torus = Mesh(
        mesh.devices.reshape(4, 2, 4, mesh.shape["fac"]), ("scen_0", "scen_1", "scen_2", "fac")
    )
    in_specs = (P(SCEN, None), P(SCEN, "fac"), P("fac", None), P("fac"))
    out_specs = (P(SCEN, "fac"), P("fac"))
    return jax.shard_map(
        on_device, mesh=torus, in_specs=in_specs, out_specs=out_specs, check_vma=False
    )
```

profile of v0, /device:TPU:0, one launch (start us, length us, event | category | flops | bytes accessed | tf_op | source)
XLA Modules:
  0.0 532.6 jit_solution(352595188754719642)
XLA Ops:
  7.2 0.0 all-gather.12.cloned.1.call-start
  7.2 10.6 %all-gather = bf16[256,1024]{1,0:T(8,128)(2,1)} all-gather(bf16[128,1024]{1,0:T(8,128)(2,1)} %param.5), channel_id=2, replica_groups=mesh['scen_0'=4,'scen_1'=2,'scen_2'=4,'fac'=4] {'scen_1'}, dimensions={0}, use_global_device_ids=true | all-gather | bytes 786432 | tf_op jit(solution)/shard_map/all_gather | solution.py:19
  17.8 0.0 all-gather.12.cloned.1.call-update
  17.9 0.0 all-gather.14.cloned.1.call-start
  17.9 33.2 %all-gather.12.cloned.1.call-done = bf16[8,128,1024]{2,1,0:T(8,128)(2,1)} async-done(((bf16[2,128,1024]{2,1,0:T(8,128)(2,1)}), bf16[8,128,1024]{2,1,0:T(8,128)(2,1)}) %all-gather.12.cloned.1.call-update) | async-done | bytes 2097168 | tf_op jit(solution)/shard_map/all_gather | solution.py:19
  51.1 0.0 all-gather.14.cloned.1.call-update
  51.1 0.0 all-gather.8.cloned.1.call-start
  51.2 84.5 %all-gather.14.cloned.1.call-done = bf16[16,2,128,1024]{3,2,1,0:T(8,128)(2,1)} async-done(((bf16[4,2,128,1024]{3,2,1,0:T(8,128)(2,1)}), bf16[16,2,128,1024]{3,2,1,0:T(8,128)(2,1)}) %all-gather.14.cloned.1.call-update) | async-done | bytes 8388624 | tf_op jit(solution)/shard_map/all_gather | solution.py:19
  135.7 0.0 copy-start.1
  135.7 8.2 %copy.9 = bf16[4,2,4,128,1024]{4,3,2,1,0:T(8,128)(2,1)} copy(bf16[4,2,4,128,1024]{4,3,1,0,2:T(8,128)(2,1)} %bitcast.12) | data formatting | bytes 16777216 | tf_op jit(solution)/shard_map/transpose | solution.py:22
  143.9 0.0 copy-done.1
  143.9 14.7 %add_convert_fusion = bf16[1024,1024]{1,0:T(8,128)(2,1)} fusion(f32[1024]{0:T(1024)S(1)} %copy-done.1, bf16[1024,4096]{1,0:T(8,128)(2,1)} %param.4, bf16[4096,1024]{1,0:T(8,128)(2,1)} %bitcast.13), kind=kOutput, calls=%fused_computation.1 | convolution fusion | flops 8592031744 | bytes 18878464 | tf_op jit(solution)/shard_map/dot_general | solution.py:42
  158.6 0.0 all-gather.8.cloned.1.call-update
  158.7 0.0 all-gather.10.cloned.1.call-start
  158.7 63.4 %all-gather.8.cloned.1.call-done = bf16[1024,4096]{1,0:T(8,128)(2,1)} async-done(((bf16[1024,1024]{1,0:T(8,128)(2,1)}), bf16[1024,4096]{1,0:T(8,128)(2,1)}) %all-gather.8.cloned.1.call-update) | async-done | bytes 8388624 | tf_op jit(solution)/shard_map/all_gather | solution.py:47
  222.1 14.8 %convolution_convert_fusion = bf16[1024,1024]{1,0:T(8,128)(2,1)} fusion(bf16[1024,4096]{1,0:T(8,128)(2,1)} %all-gather.8.cloned.1.call-done, bf16[1024,4096]{1,0:T(8,128)(2,1)} %param.6), kind=kOutput, calls=%fused_computation.2 | convolution fusion | flops 8590983168 | bytes 18874368 | tf_op jit(solution)/shard_map/dot_general | solution.py:46
  236.9 0.0 all-gather.10.cloned.1.call-update
  236.9 0.2 reduce-scatter.2.cloned.1.call-start
  237.1 61.6 %all-gather.10.cloned.1.call-done = bf16[1024,4096]{1,0:T(8,128)(2,1)} async-done(((bf16[1024,1024]{1,0:T(8,128)(2,1)}), bf16[1024,4096]{1,0:T(8,128)(2,1)}) %all-gather.10.cloned.1.call-update) | async-done | bytes 8388624 | tf_op jit(solution)/shard_map/all_gather | solution.py:53
  298.8 16.1 %fusion = f32[4096,1024]{1,0:T(8,128)} fusion(bf16[1024,4096]{1,0:T(8,128)(2,1)} %all-gather.10.cloned.1.call-done, bf16[1024,1024]{1,0:T(8,128)(2,1)} %convolution_convert_fusion), kind=kOutput, calls=%fused_computation.6 | convolution fusion | flops 8589934592 | bytes 27262976 | tf_op jit(solution)/shard_map/dot_general | solution.py:62
  314.9 0.0 reduce-scatter.2.cloned.1.call-update
  314.9 4.6 convert_reduce_fusion
  319.5 1.3 broadcast_in_dim.2
  320.7 7.3 %all-to-all-start = ((f32[32,1,4096]{2,1,0:T(1,128)}), f32[32,1,4096]{2,1,0:T(1,128)S(1)}, u32[]{:S(2)}, u32[]{:S(2)}) async-start(f32[32,1,4096]{2,1,0:T(1,128)} %broadcast_in_dim.2), calls=%async_computation.1 | async-start | bytes 1048576 | tf_op jit(solution)/shard_map/all_to_all | solution.py:32
  328.0 17.8 %all-to-all-done = f32[32,1,4096]{2,1,0:T(1,128)S(1)} async-done(((f32[32,1,4096]{2,1,0:T(1,128)}), f32[32,1,4096]{2,1,0:T(1,128)S(1)}, u32[]{:S(2)}, u32[]{:S(2)}) %all-to-all-start) | async-done | bytes 524320 | tf_op jit(solution)/shard_map/all_to_all | solution.py:32
  345.8 0.4 reduce_sum.19
  346.2 0.0 copy-start
  346.2 0.1 dynamic-slice_multiply_fusion
  346.3 177.8 %reduce-scatter.2.cloned.1.call-done = f32[128,1024]{1,0:T(8,128)} async-done(((f32[4096,1024]{1,0:T(8,128)}), f32[128,1024]{1,0:T(8,128)}) %reduce-scatter.2.cloned.1.call-update) | async-done | bytes 524304 | tf_op jit(solution)/shard_map/reduce_scatter | solution.py:61
  524.1 2.0 subtract_multiply_fusion
  526.0 0.0 copy-done
  (2 shorter events, 0.0 us)
Async XLA Ops:
  7.2 43.9 %all-gather.12.cloned.1.call-start = ((), (), s32[]{:S(2)}) async-start(), calls=%async_computation.5 | async-start | bytes 2621440 | tf_op jit(solution)/shard_map/all_gather | solution.py:19
  17.9 117.8 %all-gather.14.cloned.1.call-start = ((), (), s32[]{:S(2)}) async-start(), calls=%async_computation.6 | async-start | bytes 10485760 | tf_op jit(solution)/shard_map/all_gather | solution.py:19
  51.1 171.0 %all-gather.8.cloned.1.call-start = ((), (), s32[]{:S(2)}) async-start(), calls=%async_computation.2 | async-start | bytes 10485760 | tf_op jit(solution)/shard_map/all_gather | solution.py:47
  135.7 8.2 %copy-start.1 = (f32[1024]{0:T(1024)S(1)}, f32[1024]{0:T(1024)}, u32[]{:S(2)}) copy-start(f32[1024]{0:T(1024)} %param.7) | copy-start | bytes 12292
  158.7 140.1 %all-gather.10.cloned.1.call-start = ((), (), s32[]{:S(2)}) async-start(), calls=%async_computation.3 | async-start | bytes 10485760 | tf_op jit(solution)/shard_map/all_gather | solution.py:53
  236.9 287.2 %reduce-scatter.2.cloned.1.call-start = ((), (), s32[]{:S(2)}) async-start(), calls=%async_computation.4 | async-start | bytes 17301504 | tf_op jit(solution)/shard_map/reduce_scatter | solution.py:61
  320.7 25.1 %all-to-all-start = ((f32[32,1,4096]{2,1,0:T(1,128)}), f32[32,1,4096]{2,1,0:T(1,128)S(1)}, u32[]{:S(2)}, u32[]{:S(2)}) async-start(f32[32,1,4096]{2,1,0:T(1,128)} %broadcast_in_dim.2), calls=%async_computation.1 | async-start | bytes 1048576 | tf_op jit(solution)/shard_map/all_to_all | solution.py:32
  346.2 179.8 %copy-start = (f32[1024]{0:T(1024)}, f32[1024]{0:T(1024)S(1)}, u32[]{:S(2)}) copy-start(f32[1024]{0:T(1024)S(1)} %dynamic_slice.7) | copy-start | bytes 12292
Sparse Core Ops, SparseCore 0:
  18.0 33.0 all-gather.11
  52.8 82.8 all-gather.13
  158.8 63.2 all-gather.7
  237.0 61.6 all-gather.9
  315.0 209.0 reduce-scatter.1
where the time goes:
time: 533 us
  waiting for transfers between devices  438 us (82%)
  matrix products  45.6 us (9%)
  between operations  13.8 us (3%)
  blocking collectives  10.6 us (2%)
  local copies, waits for them, and re-layouts  9.51 us (2%)
  starting transfers between devices  7.64 us (1%)
  other arithmetic  6.96 us (1%)
    reduce_scatter x1, waiting for transfers between devices, on_device(): lax.psum_scatter(lax.dot_general(gathered, pnl, (((0,), (0,)), ((), ())),...  178 us
    all_gather x2, waiting for transfers between devices, gather_in_order(): tiles = lax.all_gather(tiles, axes[k])  118 us
    all_gather x1, waiting for transfers between devices, on_device(): lax.all_gather(shocks, 'fac', axis=1, tiled=True)  63.4 us
    all_gather x1, waiting for transfers between devices, on_device(): gathered = lax.all_gather(pnl, 'fac', axis=1, tiled=True)  61.6 us
    all_to_all x1, waiting for transfers between devices, from_everyone(): return lax.all_to_all(copies, axis, split_axis=0, concat_axis=0, tiled=True)  17.8 us
    dot_general x1, matrix products, on_device(): lax.dot_general(gathered, pnl, (((0,), (0,)), ((), ())), preferred_elemen...  16.1 us
    dot_general x1, matrix products, on_device(): lax.dot_general(lax.all_gather(shocks, 'fac', axis=1, tiled=True), exposu...  14.8 us
    dot_general x1, matrix products, on_device(): jnp.dot(scenario_draws, whole_of(cholesky, SCEN, (1, 0, 2), 0), preferred...  14.7 us
  transfers between devices with their start and end apart: 6, of which 6 were waited for; matrix products, arithmetic and copies ran while one was open for 1% of the time, Pallas kernels for 0%

commit v1 on v0

--- a/solution.py
+++ b/solution.py
@@ -1,10 +1,26 @@
+import functools
 import jax
 import jax.numpy as jnp
 from jax import lax
 from jax.sharding import Mesh
 from jax.sharding import PartitionSpec as P
+from jax.lax import all_to_all, axis_size
 
 SCEN = ("scen_0", "scen_1", "scen_2")
+
+
+def wrap_things_on(xx, across):
+    d_next = all_to_all(
+        jnp.stack([xx for _ in range(axis_size(across))], axis=0),
+        axis_name=across,
+        split_axis=0,
+        concat_axis=0,
+    )
+    newest = jnp.concatenate(d_next, axis=1)
+    return newest
+
+
+fit_the_sectors = functools.partial(wrap_things_on, across="fac")
 
 
 def in_order(tiles, dim):
@@ -44,7 +60,7 @@
     )
     shocks = (mixed + drift[None, :]).astype(jnp.bfloat16)
     pnl_acc = lax.dot_general(
-        lax.all_gather(shocks, "fac", axis=1, tiled=True),
+        fit_the_sectors(shocks),
         exposures,
         (((1,), (1,)), ((), ())),
         preferred_element_type=jnp.float32,

time: 533 us -> 569 us (1.068)
  blocking collectives: 10.6 us -> 109 us
  waiting for transfers between devices: 438 us -> 374 us
    all_to_all x0 -> x1, blocking collectives: none -> 98.7 us  [wrap_things_on(): all_to_all(jnp.stack([xx for _ in range(axis_size(across))], axis=0), axi...]
    all_gather x1 -> x0, waiting for transfers between devices: 63.4 us -> none  [on_device(): lax.all_gather(shocks, 'fac', axis=1, tiled=True)]
  transfers between devices with their start and end apart: 6 -> 5, of which waited for: 6 -> 5; matrix products, arithmetic and copies ran while one was open for 1% -> 1% of each run, Pallas kernels for 0% -> 0%
where the time goes in v1:
time: 569 us; the launch traced here: 568 us
  waiting for transfers between devices  374 us (66%)
  blocking collectives  109 us (19%)
  matrix products  43.2 us (8%)
  between operations  13.8 us (2%)
  local copies, waits for them, and re-layouts  13.5 us (2%)
  starting transfers between devices  7.59 us (1%)
  other arithmetic  6.96 us (1%)
    reduce_scatter x1, waiting for transfers between devices, on_device(): lax.psum_scatter(lax.dot_general(gathered, pnl, (((0,), (0,)), ((), ())),...  178 us
    all_gather x2, waiting for transfers between devices, gather_in_order(): tiles = lax.all_gather(tiles, axes[k])  118 us
    all_to_all x1, blocking collectives, wrap_things_on(): all_to_all(jnp.stack([xx for _ in range(axis_size(across))], axis=0), axi...  98.7 us
    all_gather x1, waiting for transfers between devices, on_device(): gathered = lax.all_gather(pnl, 'fac', axis=1, tiled=True)  60.8 us
    all_to_all x1, waiting for transfers between devices, from_everyone(): return lax.all_to_all(copies, axis, split_axis=0, concat_axis=0, tiled=True)  17.8 us
    dot_general x1, matrix products, on_device(): lax.dot_general(gathered, pnl, (((0,), (0,)), ((), ())), preferred_elemen...  16.2 us
    dot_general x1, matrix products, on_device(): jnp.dot(scenario_draws, whole_of(cholesky, SCEN, (1, 0, 2), 0), preferred...  14.7 us
    dot_general x1, matrix products, on_device(): lax.dot_general(fit_the_sectors(shocks), exposures, (((1,), (1,)), ((), (...  12.3 us
  transfers between devices with their start and end apart: 5, of which 5 were waited for; matrix products, arithmetic and copies ran while one was open for 1% of the time, Pallas kernels for 0%

profile of v1, /device:TPU:0, one launch (start us, length us, event | category | flops | bytes accessed | tf_op | source)
XLA Modules:
  0.0 568.4 jit_solution(17965379266684886791)
XLA Ops:
  7.2 0.0 all-gather.9.cloned.1.call-start
  7.2 10.6 %all-gather = bf16[256,1024]{1,0:T(8,128)(2,1)} all-gather(bf16[128,1024]{1,0:T(8,128)(2,1)} %param.5), channel_id=2, replica_groups=mesh['scen_0'=4,'scen_1'=2,'scen_2'=4,'fac'=4] {'scen_1'}, dimensions={0}, use_global_device_ids=true | all-gather | bytes 786432 | tf_op jit(solution)/shard_map/all_gather | solution.py:35
  17.8 0.0 all-gather.9.cloned.1.call-update
  17.9 0.0 all-gather.11.cloned.1.call-start
  17.9 33.2 %all-gather.9.cloned.1.call-done = bf16[8,128,1024]{2,1,0:T(8,128)(2,1)} async-done(((bf16[2,128,1024]{2,1,0:T(8,128)(2,1)}), bf16[8,128,1024]{2,1,0:T(8,128)(2,1)}) %all-gather.9.cloned.1.call-update) | async-done | bytes 2097168 | tf_op jit(solution)/shard_map/all_gather | solution.py:35
  51.1 0.0 all-gather.11.cloned.1.call-update
  51.1 0.0 all-gather.7.cloned.1.call-start
  51.2 84.5 %all-gather.11.cloned.1.call-done = bf16[16,2,128,1024]{3,2,1,0:T(8,128)(2,1)} async-done(((bf16[4,2,128,1024]{3,2,1,0:T(8,128)(2,1)}), bf16[16,2,128,1024]{3,2,1,0:T(8,128)(2,1)}) %all-gather.11.cloned.1.call-update) | async-done | bytes 8388624 | tf_op jit(solution)/shard_map/all_gather | solution.py:35
  135.7 0.0 copy-start.1
  135.7 8.2 %copy.13 = bf16[4,2,4,128,1024]{4,3,2,1,0:T(8,128)(2,1)} copy(bf16[4,2,4,128,1024]{4,3,1,0,2:T(8,128)(2,1)} %bitcast.15) | data formatting | bytes 16777216 | tf_op jit(solution)/shard_map/transpose | solution.py:38
  143.9 0.0 copy-done.1
  143.9 14.7 %add_convert_fusion = bf16[1024,1024]{1,0:T(8,128)(2,1)} fusion(f32[1024]{0:T(1024)S(1)} %copy-done.1, bf16[1024,4096]{1,0:T(8,128)(2,1)} %param.4, bf16[4096,1024]{1,0:T(8,128)(2,1)} %bitcast.16), kind=kOutput, calls=%fused_computation.1 | convolution fusion | flops 8592031744 | bytes 18878464 | tf_op jit(solution)/shard_map/dot_general | solution.py:58
  158.6 2.9 copy.14
  161.5 1.2 stack.2
  162.7 98.7 %all_to_all.11 = bf16[4,1024,1024]{1,2,0:T(8,128)(2,1)S(1)} all-to-all(bf16[4,1024,1024]{1,2,0:T(8,128)(2,1)S(1)} %stack.2), channel_id=1, replica_groups=mesh['scen_0'=4,'scen_1'=2,'scen_2'=4,'fac'=4] {'fac'}, dimensions={0} | all-to-all | bytes 16777216 | tf_op jit(solution)/shard_map/all_to_all | solution.py:13
  261.3 12.3 %convolution_convert_fusion = bf16[1024,1024]{1,0:T(8,128)(2,1)} fusion(bf16[1024,4096]{0,1:T(8,128)(2,1)S(1)} %bitcast.17, bf16[1024,4096]{1,0:T(8,128)(2,1)} %param.6), kind=kOutput, calls=%fused_computation.2 | convolution fusion | flops 8590983168 | bytes 18874368 | tf_op jit(solution)/shard_map/dot_general | solution.py:62
  273.7 0.0 all-gather.7.cloned.1.call-update
  273.7 0.2 reduce-scatter.2.cloned.1.call-start
  273.9 60.8 %all-gather.7.cloned.1.call-done = bf16[1024,4096]{1,0:T(8,128)(2,1)} async-done(((bf16[1024,1024]{1,0:T(8,128)(2,1)}), bf16[1024,4096]{1,0:T(8,128)(2,1)}) %all-gather.7.cloned.1.call-update) | async-done | bytes 8388624 | tf_op jit(solution)/shard_map/all_gather | solution.py:69
  334.7 16.2 %fusion = f32[4096,1024]{1,0:T(8,128)} fusion(bf16[1024,4096]{1,0:T(8,128)(2,1)} %all-gather.7.cloned.1.call-done, bf16[1024,1024]{1,0:T(8,128)(2,1)} %convolution_convert_fusion), kind=kOutput, calls=%fused_computation.6 | convolution fusion | flops 8589934592 | bytes 27262976 | tf_op jit(solution)/shard_map/dot_general | solution.py:78
  350.9 0.0 reduce-scatter.2.cloned.1.call-update
  350.9 4.6 convert_reduce_fusion
  355.5 1.3 broadcast_in_dim.2
  356.7 7.3 %all-to-all-start.1 = ((f32[32,1,4096]{2,1,0:T(1,128)}), f32[32,1,4096]{2,1,0:T(1,128)S(1)}, u32[]{:S(2)}, u32[]{:S(2)}) async-start(f32[32,1,4096]{2,1,0:T(1,128)} %broadcast_in_dim.2), calls=%async_computation.2 | async-start | bytes 1048576 | tf_op jit(solution)/shard_map/all_to_all | solution.py:48
  364.0 17.8 %all-to-all-done.1 = f32[32,1,4096]{2,1,0:T(1,128)S(1)} async-done(((f32[32,1,4096]{2,1,0:T(1,128)}), f32[32,1,4096]{2,1,0:T(1,128)S(1)}, u32[]{:S(2)}, u32[]{:S(2)}) %all-to-all-start.1) | async-done | bytes 524320 | tf_op jit(solution)/shard_map/all_to_all | solution.py:48
  381.8 0.4 reduce_sum.19
  382.2 0.0 copy-start
  382.2 0.1 dynamic-slice_multiply_fusion
  382.3 177.7 %reduce-scatter.2.cloned.1.call-done = f32[128,1024]{1,0:T(8,128)} async-done(((f32[4096,1024]{1,0:T(8,128)}), f32[128,1024]{1,0:T(8,128)}) %reduce-scatter.2.cloned.1.call-update) | async-done | bytes 524304 | tf_op jit(solution)/shard_map/reduce_scatter | solution.py:77
  559.9 2.0 subtract_multiply_fusion
  561.9 0.0 copy-done
  (2 shorter events, 0.0 us)
Async XLA Ops:
  7.2 43.9 %all-gather.9.cloned.1.call-start = ((), (), s32[]{:S(2)}) async-start(), calls=%async_computation.5 | async-start | bytes 2621440 | tf_op jit(solution)/shard_map/all_gather | solution.py:35
  17.9 117.8 %all-gather.11.cloned.1.call-start = ((), (), s32[]{:S(2)}) async-start(), calls=%async_computation.6 | async-start | bytes 10485760 | tf_op jit(solution)/shard_map/all_gather | solution.py:35
  51.1 283.6 %all-gather.7.cloned.1.call-start = ((), (), s32[]{:S(2)}) async-start(), calls=%async_computation.3 | async-start | bytes 10485760 | tf_op jit(solution)/shard_map/all_gather | solution.py:69
  135.7 8.2 %copy-start.1 = (f32[1024]{0:T(1024)S(1)}, f32[1024]{0:T(1024)}, u32[]{:S(2)}) copy-start(f32[1024]{0:T(1024)} %param.7) | copy-start | bytes 12292
  273.7 286.2 %reduce-scatter.2.cloned.1.call-start = ((), (), s32[]{:S(2)}) async-start(), calls=%async_computation.4 | async-start | bytes 17301504 | tf_op jit(solution)/shard_map/reduce_scatter | solution.py:77
  356.7 25.1 %all-to-all-start.1 = ((f32[32,1,4096]{2,1,0:T(1,128)}), f32[32,1,4096]{2,1,0:T(1,128)S(1)}, u32[]{:S(2)}, u32[]{:S(2)}) async-start(f32[32,1,4096]{2,1,0:T(1,128)} %broadcast_in_dim.2), calls=%async_computation.2 | async-start | bytes 1048576 | tf_op jit(solution)/shard_map/all_to_all | solution.py:48
  382.2 179.7 %copy-start = (f32[1024]{0:T(1024)}, f32[1024]{0:T(1024)S(1)}, u32[]{:S(2)}) copy-start(f32[1024]{0:T(1024)S(1)} %dynamic_slice.7) | copy-start | bytes 12292
Sparse Core Ops, SparseCore 0:
  18.0 33.0 all-gather.8
  52.7 82.8 all-gather.10
  273.8 60.8 all-gather.6
  351.0 208.8 reduce-scatter.1
